TPU v7x, 32 devices: a whole 2x2x4 slice. The times are simulated.
32 devices in a mesh: paths: 4 (over x, core), cpty: 8 (over z, y).
Axes of the slice: x: 2, y: 2, z: 4, core: 2. Of those that a mesh axis runs over, the one named last changes fastest.
Arguments:
- factors: bfloat16 [64, 6144], P(None, 'paths'), may hold values from -6 to 6
- loadings: bfloat16 [64, 16384], P(None, 'cpty'), may hold values from -2 to 2
- notional: bfloat16 [16384], P('cpty'), may hold values from 0.25 to 0.796875
- strike: bfloat16 [16384], P('cpty'), may hold values from 2 to 8
- curvature: bfloat16 [16384], P('cpty'), may hold values from 1 to 3
- trade_cpty: int32 [16384], P('cpty'), may hold values from 0 to 1023, as said below
Outputs:
- exposure: bfloat16 [6144, 1024], P('paths', 'cpty')
- moment: float32 [1024, 1024], P('paths', 'cpty')
Inputs may be any that keep to these rules, and one draw needn't show every extreme that they name: `trade_cpty`: of the trades in the book of one index of cpty, at most 512 belong to the counterparties numbered k * 128 to (k + 1) * 128 - 1 for any k; in every draw some such k receives exactly 512 from every book.
All inputs are finite; a program needn't handle non-finite values.
Results may differ from a plain program's by a relative error of at most 0.0064.
Values may be sent and summed in bfloat16 or wider, within the bound.
No kernel may reach another device: no remote copies, remote signals or barrier semaphores. Data moves between devices by JAX's collectives and lax.ppermute only.
A program may use at most 128 MiB of HBM per device.

v0:
```python
import jax
import jax.numpy as jnp
from jax import lax
from jax.sharding import PartitionSpec as P

CP_DEV = 128


def price_trades(drivers, loading_cols, trade_terms):
    linear = jnp.dot(drivers, loading_cols, preferred_element_type=jnp.float32)
    terms_wide = trade_terms.astype(jnp.float32)
    value = terms_wide[0] * (linear + terms_wide[2] * jnp.tanh(linear - terms_wide[1]))
    return value.astype(jnp.bfloat16)


def on_device(factors, loadings, notional, strike, curvature, trade_cpty):
    groups = lax.axis_size("cpty")
    own_index = lax.axis_index("cpty")
    trades = loadings.shape[1]
    slot_size = 2 * trades // groups
    owners = trade_cpty // CP_DEV
    marked = (owners[:, None] == jnp.arange(groups, dtype=jnp.int32)[None, :]).astype(jnp.int32)
    ranking = jnp.sum((jnp.cumsum(marked, axis=0) - marked) * marked, axis=1)
    target = owners * slot_size + ranking
    chosen = (
        jnp.zeros((groups * slot_size,), jnp.int32)
        .at[target]
        .set(jnp.arange(trades, dtype=jnp.int32))
    )
    filled = jnp.zeros((groups * slot_size,), jnp.bool_).at[target].set(True)
    labels = jnp.where(filled, trade_cpty[chosen], -1)[None, :]
    drivers = jnp.transpose(factors)
    trade_terms = jnp.stack([notional, strike, curvature])
    described = jnp.concatenate([loadings, trade_terms], axis=0)
    packed = jnp.where(
        filled[None, :], jnp.take(described, chosen, axis=1), jnp.zeros((), jnp.bfloat16)
    )
    received, arrived_ids = (
        lax.all_to_all(packed, "cpty", split_axis=1, concat_axis=1, tiled=True),
        lax.all_to_all(labels, "cpty", split_axis=1, concat_axis=1, tiled=True),
    )
    factor_count = loadings.shape[0]
    arrived = price_trades(drivers, received[:factor_count], received[factor_count:])
    local_ids = arrived_ids[0] - own_index * CP_DEV
    onehot = (local_ids[:, None] == jnp.arange(CP_DEV, dtype=jnp.int32)[None, :]).astype(
        jnp.bfloat16
    )
    netted = jnp.dot(arrived, onehot, preferred_element_type=jnp.float32)
    exposure = jnp.maximum(netted, 0.0).astype(jnp.bfloat16)
    everyone = lax.all_gather(exposure, "cpty", axis=1, tiled=True)
    path_total = exposure.shape[0] * lax.axis_size("paths")
    moment = (
        lax.psum_scatter(
            jnp.einsum("pa,pb->ab", everyone, exposure, preferred_element_type=jnp.float32),
            "paths",
            scatter_dimension=0,
            tiled=True,
        )
        / path_total
    )
    return (exposure, moment)


def solution(mesh):
    in_specs = (P(None, "paths"), P(None, "cpty"), P("cpty"), P("cpty"), P("cpty"), P("cpty"))
    out_specs = (P("paths", "cpty"), P("paths", "cpty"))
    return jax.shard_map(
        on_device, mesh=mesh, in_specs=in_specs, out_specs=out_specs, check_vma=False
    )
```

profile of v0, /device:TPU:0, one launch (start us, length us, event | category | flops | bytes accessed | tf_op | source)
XLA Modules:
  0.0 204.9 jit_solution(14715116246756037690)
XLA Ops:
  7.2 0.8 add_select_fusion
  8.0 2.3 %reduce-window.6 = s32[8,16,128]{2,1,0:T(8,128)S(1)} reduce-window(s32[8,16,128]{2,1,0:T(8,128)S(1)} %fusion.14, s32[]{:T(128)} %constant.24.clone.1), window={size=1x1x128 pad=0_0x0_0x127_0}, to_apply=%region_0.1 | reduce-window | flops 2080768 | bytes 131076 | tf_op jit(solution)/shard_map/reduce-window
  10.3 0.3 slice_reduce_fusion
  10.9 0.7 compare_select_fusion.1
  11.6 8.1 %scatter_custom_fusion.1 = s32[4096]{0:T(1024)S(1)} fusion(s32[2048]{0:T(1024)S(1)} %compare_select_fusion.1, s32[2048]{0:T(1024)S(1)} %iota.15, s32[]{:T(128)} %constant.24.clone.1), kind=kCustom, calls=%fused_computation.43 | custom fusion | bytes 16388 | tf_op jit(solution)/shard_map/scatter | solution.py:28
  19.7 23.0 %gather_fusion.1 = s32[4096]{0:T(1024)S(1)} fusion(s32[2048]{0:T(1024)S(1)} %copy-done.1, s32[4096]{0:T(1024)S(1)} %fusion.15), kind=kCustom, calls=%fused_computation.1 | custom fusion | bytes 49152 | tf_op jit(solution)/shard_map/gather | solution.py:31
  42.8 9.1 %scatter_custom_fusion = pred[4096]{0:T(1024)(128)(4,1)S(1)} fusion(s32[2048]{0:T(1024)S(1)} %compare_select_fusion.1, pred[2048]{0:T(1024)(128)(4,1)S(1)} %broadcast.49, pred[]{:T(512)} %constant.22.clone.1), kind=kCustom, calls=%fused_computation.47 | custom fusion | bytes 4097 | tf_op jit(solution)/shard_map/scatter | solution.py:30
  51.9 0.6 broadcast_select_fusion
  52.5 7.3 %all-to-all-start.1 = ((s32[1,8,512]{2,0,1:T(1,128)}), s32[1,8,512]{2,0,1:T(1,128)S(1)}, u32[]{:S(2)}, u32[]{:S(2)}) async-start(s32[1,8,512]{2,0,1:T(1,128)} %bitcast.8), calls=%async_computation.1 | async-start | bytes 32768 | tf_op jit(solution)/shard_map/all_to_all | solution.py:40
  60.2 0.3 stack.12
  60.5 0.3 stack.13
  60.9 0.3 stack.14
  61.2 0.7 pad_maximum_fusion
  61.9 12.1 %gather_fusion = bf16[4096,67]{1,0:T(8,128)(2,1)S(1)} fusion(bf16[67,2048]{0,1:T(8,128)(2,1)S(1)} %pad_maximum_fusion, s32[4096]{0:T(1024)S(1)} %fusion.15), kind=kCustom, calls=%fused_computation | custom fusion | bytes 1114112 | tf_op jit(solution)/shard_map/jit(_take)/gather | solution.py:36
  74.1 0.6 copy.23
  74.6 0.9 select_select_fusion
  75.5 6.0 %all-to-all-start = ((bf16[67,8,512]{2,0,1:T(8,128)(2,1)}), bf16[67,8,512]{2,0,1:T(8,128)(2,1)S(1)}, u32[]{:S(2)}, u32[]{:S(2)}) async-start(bf16[67,8,512]{2,0,1:T(8,128)(2,1)} %select_select_fusion), calls=%async_computation | async-start | bytes 1179648 | tf_op jit(solution)/shard_map/all_to_all | solution.py:39
  81.6 0.9 iota_compare_fusion.7
  82.5 14.4 %all-to-all-done = bf16[67,8,512]{2,0,1:T(8,128)(2,1)S(1)} async-done(((bf16[67,8,512]{2,0,1:T(8,128)(2,1)}), bf16[67,8,512]{2,0,1:T(8,128)(2,1)S(1)}, u32[]{:S(2)}, u32[]{:S(2)}) %all-to-all-start) | async-done | bytes 548896 | tf_op jit(solution)/shard_map/all_to_all | solution.py:39
  97.1 13.8 %fusion.9 = bf16[1536,128]{1,0:T(8,128)(2,1)} fusion(bf16[64,4096]{1,0:T(8,128)(2,1)S(1)} %bitcast.70, bf16[64,1536]{1,0:T(8,128)(2,1)S(1)} %copy-done, f32[4096]{0:T(1024)S(1)} %bitcast.75, f32[4096]{0:T(1024)S(1)} %bitcast.76, f32[4096]{0:T(1024)S(1)} %bitcast.74, pred[4096,128]{1,0:T(32,128)(4,1)S(1)} %iota_compare_fusion.7), kind=kOutput, calls=%fused_computation.15 | convolution fusion | flops 2447769600 | bytes 1687552 | tf_op jit(solution)/shard_map/dot_general | solution.py:48
  110.9 61.8 %all-gather.2.cloned.1.call-done = bf16[1536,1024]{1,0:T(8,128)(2,1)} async-done(((bf16[1536,128]{1,0:T(8,128)(2,1)}), bf16[1536,1024]{1,0:T(8,128)(2,1)}) %all-gather.2.cloned.1.call-update) | async-done | bytes 3145744 | tf_op jit(solution)/shard_map/all_gather | solution.py:50
  172.7 3.7 %fusion.24 = f32[1024,128]{1,0:T(8,128)} fusion(bf16[1536,1024]{1,0:T(8,128)(2,1)} %all-gather.2.cloned.1.call-done, bf16[1536,128]{1,0:T(8,128)(2,1)} %fusion.9), kind=kOutput, calls=%fused_computation.51 | convolution fusion | flops 402653184 | bytes 4063232 | tf_op jit(solution)/shard_map/pa,pb->ab/dot_general | solution.py:54
  176.5 20.0 %reduce-scatter.2.cloned.1.call-done = f32[256,128]{1,0:T(8,128)} async-done(((f32[1024,128]{1,0:T(8,128)}), f32[256,128]{1,0:T(8,128)}) %reduce-scatter.2.cloned.1.call-update) | async-done | bytes 131088 | tf_op jit(solution)/shard_map/reduce_scatter | solution.py:53
  196.4 1.6 broadcast_multiply_fusion
  (33 shorter events, 0.9 us)
Async XLA Ops:
  7.2 89.9 %copy-start = (bf16[64,1536]{1,0:T(8,128)(2,1)S(1)}, bf16[64,1536]{1,0:T(8,128)(2,1)}, u32[]{:S(2)}) copy-start(bf16[64,1536]{1,0:T(8,128)(2,1)} %param.6) | copy-start | bytes 589828
  7.2 12.5 %copy-start.1 = (s32[2048]{0:T(1024)S(1)}, s32[2048]{0:T(1024)}, u32[]{:S(2)}) copy-start(s32[2048]{0:T(1024)} %param.11) | copy-start | bytes 24580
  19.7 40.2 %copy-start.2 = (bf16[64,2048]{1,0:T(8,128)(2,1)S(1)}, bf16[64,2048]{1,0:T(8,128)(2,1)}, u32[]{:S(2)}) copy-start(bf16[64,2048]{1,0:T(8,128)(2,1)} %param.7) | copy-start | bytes 786436
  19.7 40.5 %copy-start.3 = (bf16[2048]{0:T(1024)(128)(2,1)S(1)}, bf16[2048]{0:T(1024)(128)(2,1)}, u32[]{:S(2)}) copy-start(bf16[2048]{0:T(1024)(128)(2,1)} %param.8) | copy-start | bytes 12292
  19.7 40.8 %copy-start.4 = (bf16[2048]{0:T(1024)(128)(2,1)S(1)}, bf16[2048]{0:T(1024)(128)(2,1)}, u32[]{:S(2)}) copy-start(bf16[2048]{0:T(1024)(128)(2,1)} %param.9) | copy-start | bytes 12292
  19.7 41.2 %copy-start.5 = (bf16[2048]{0:T(1024)(128)(2,1)S(1)}, bf16[2048]{0:T(1024)(128)(2,1)}, u32[]{:S(2)}) copy-start(bf16[2048]{0:T(1024)(128)(2,1)} %param.10) | copy-start | bytes 12292
  52.5 23.0 %all-to-all-start.1 = ((s32[1,8,512]{2,0,1:T(1,128)}), s32[1,8,512]{2,0,1:T(1,128)S(1)}, u32[]{:S(2)}, u32[]{:S(2)}) async-start(s32[1,8,512]{2,0,1:T(1,128)} %bitcast.8), calls=%async_computation.1 | async-start | bytes 32768 | tf_op jit(solution)/shard_map/all_to_all | solution.py:40
  75.5 21.4 %all-to-all-start = ((bf16[67,8,512]{2,0,1:T(8,128)(2,1)}), bf16[67,8,512]{2,0,1:T(8,128)(2,1)S(1)}, u32[]{:S(2)}, u32[]{:S(2)}) async-start(bf16[67,8,512]{2,0,1:T(8,128)(2,1)} %select_select_fusion), calls=%async_computation | async-start | bytes 1179648 | tf_op jit(solution)/shard_map/all_to_all | solution.py:39
  81.5 91.2 %all-gather.2.cloned.1.call-start = ((), (), s32[]{:S(2)}) async-start(), calls=%async_computation.3 | async-start | bytes 3538944 | tf_op jit(solution)/shard_map/all_gather | solution.py:50
  110.9 85.6 %reduce-scatter.2.cloned.1.call-start = ((), (), s32[]{:S(2)}) async-start(), calls=%async_computation.4 | async-start | bytes 655360 | tf_op jit(solution)/shard_map/reduce_scatter | solution.py:53
Sparse Core Ops, SparseCore 0:
  111.0 61.6 all-gather.1
  176.6 19.7 reduce-scatter.1
where the time goes:
time: 205 us
  waiting for transfers between devices  96.2 us (47%)
  local copies, waits for them, and re-layouts  54.7 us (27%)
  matrix products  17.5 us (9%)
  between operations  14.3 us (7%)
  starting transfers between devices  13.4 us (7%)
  other arithmetic  8.76 us (4%)
    all_gather x1, waiting for transfers between devices, on_device(): everyone = lax.all_gather(exposure, 'cpty', axis=1, tiled=True)  61.8 us
    gather x1, local copies, waits for them, and re-layouts, on_device(): labels = jnp.where(filled, trade_cpty[chosen], -1)[None, :]  23 us
    reduce_scatter x1, waiting for transfers between devices, on_device(): lax.psum_scatter(jnp.einsum('pa,pb->ab', everyone, exposure, preferred_el...  20 us
    all_to_all x1, waiting for transfers between devices, on_device(): lax.all_to_all(packed, 'cpty', split_axis=1, concat_axis=1, tiled=True)  14.4 us
    dot_general x1, matrix products, on_device(): netted = jnp.dot(arrived, onehot, preferred_element_type=jnp.float32)  13.8 us
    gather x2, local copies, waits for them, and re-layouts, on_device(): jnp.take(described, chosen, axis=1)  12.7 us
    scatter x1, local copies, waits for them, and re-layouts, on_device(): filled = jnp.zeros((groups * slot_size,), jnp.bool_).at[target].set(True)  9.13 us
    scatter x1, local copies, waits for them, and re-layouts, on_device(): chosen = jnp.zeros((groups * slot_size,), jnp.int32).at[target].set(jnp.a...  8.06 us
  transfers between devices with their start and end apart: 4, of which 3 were waited for; matrix products, arithmetic and copies ran while one was open for 8% of the time, Pallas kernels for 0%

commit v1 on v0

--- a/solution.py
+++ b/solution.py
@@ -4,6 +4,31 @@
 from jax.sharding import PartitionSpec as P
 
 CP_DEV = 128
+
+
+def laid_out(blocks, dim):
+    lengths = list(blocks.shape[1:])
+    lengths[dim] *= blocks.shape[0]
+    return jnp.moveaxis(blocks, 0, dim).reshape(lengths)
+
+
+def ring_apply(shard, axis, dim, apply, out_dim):
+    size, mine, rows = (lax.axis_size(axis), lax.axis_index(axis), shard.shape[dim])
+    right = [(i, (i + 1) % size) for i in range(size)]
+    backward = [(i, (i - 1) % size) for i in range(size)]
+    half = size // 2
+    blocks = {}
+    from_left = from_right = shard
+    for step in range(half + 1):
+        next_left = lax.ppermute(from_left, axis, right) if step < half else None
+        next_right = lax.ppermute(from_right, axis, backward) if step < size - half - 1 else None
+        blocks[-step] = apply(from_left, (mine - step) % size * rows)
+        if 0 < step < size - half:
+            blocks[step] = apply(from_right, (mine + step) % size * rows)
+        from_left, from_right = (next_left, next_right)
+    blocks = jnp.stack([blocks[k] for k in sorted(blocks)])
+    blocks = blocks[(jnp.arange(size) - mine + half) % size]
+    return laid_out(blocks, out_dim)
 
 
 def price_trades(drivers, loading_cols, trade_terms):
@@ -47,11 +72,18 @@
     )
     netted = jnp.dot(arrived, onehot, preferred_element_type=jnp.float32)
     exposure = jnp.maximum(netted, 0.0).astype(jnp.bfloat16)
-    everyone = lax.all_gather(exposure, "cpty", axis=1, tiled=True)
     path_total = exposure.shape[0] * lax.axis_size("paths")
     moment = (
         lax.psum_scatter(
-            jnp.einsum("pa,pb->ab", everyone, exposure, preferred_element_type=jnp.float32),
+            ring_apply(
+                exposure,
+                "cpty",
+                1,
+                lambda own_block, offset: jnp.einsum(
+                    "pa,pb->ab", own_block, exposure, preferred_element_type=jnp.float32
+                ),
+                0,
+            ),
             "paths",
             scatter_dimension=0,
             tiled=True,

time: 205 us -> 207 us (level)
  starting transfers between devices: 13.4 us -> 29.4 us
  waiting for transfers between devices: 96.2 us -> 82.7 us
    all_gather x1 -> x0, waiting for transfers between devices: 61.8 us -> none  [on_device(): everyone = lax.all_gather(exposure, 'cpty', axis=1, tiled=True)]
    ppermute x0 -> x7, waiting for transfers between devices: none -> 47 us  [the longest x4 46.5 us: ring_apply(): next_left = lax.ppermute(from_left, axis, right) if step < half else None]
    ppermute x0 -> x7, starting transfers between devices: none -> 16.1 us  [the longest x3 9.64 us: ring_apply(): lax.ppermute(from_right, axis, backward)]
  transfers between devices with their start and end apart: 4 -> 10, of which waited for: 3 -> 7; matrix products, arithmetic and copies ran while one was open for 8% -> 9% of each run, Pallas kernels for 0% -> 0%
where the time goes in v1:
time: 207 us
  waiting for transfers between devices  82.7 us (40%)
  local copies, waits for them, and re-layouts  56.1 us (27%)
  starting transfers between devices  29.4 us (14%)
  matrix products  15.7 us (8%)
  between operations  14.4 us (7%)
  other arithmetic  8.81 us (4%)
    ppermute x4, waiting for transfers between devices, ring_apply(): next_left = lax.ppermute(from_left, axis, right) if step < half else None  46.5 us
    gather x1, local copies, waits for them, and re-layouts, on_device(): labels = jnp.where(filled, trade_cpty[chosen], -1)[None, :]  23 us
    reduce_scatter x1, waiting for transfers between devices, on_device(): lax.psum_scatter(ring_apply(exposure, 'cpty', 1, lambda own_block, offset...  21.3 us
    all_to_all x1, waiting for transfers between devices, on_device(): lax.all_to_all(packed, 'cpty', split_axis=1, concat_axis=1, tiled=True)  14.4 us
    dot_general x1, matrix products, on_device(): netted = jnp.dot(arrived, onehot, preferred_element_type=jnp.float32)  13.2 us
    gather x2, local copies, waits for them, and re-layouts, on_device(): jnp.take(described, chosen, axis=1)  12.7 us
    ppermute x3, starting transfers between devices, ring_apply(): lax.ppermute(from_right, axis, backward)  9.64 us
    scatter x1, local copies, waits for them, and re-layouts, on_device(): filled = jnp.zeros((groups * slot_size,), jnp.bool_).at[target].set(True)  9.13 us
  transfers between devices with their start and end apart: 10, of which 7 were waited for; matrix products, arithmetic and copies ran while one was open for 9% of the time, Pallas kernels for 0%

profile of v1, /device:TPU:0, one launch (start us, length us, event | category | flops | bytes accessed | tf_op | source)
XLA Modules:
  0.0 207.1 jit_solution(1001644871289091661)
XLA Ops:
  8.0 2.3 %reduce-window.6 = s32[8,16,128]{2,1,0:T(8,128)S(1)} reduce-window(s32[8,16,128]{2,1,0:T(8,128)S(1)} %fusion.22, s32[]{:T(128)} %constant.38.clone.1), window={size=1x1x128 pad=0_0x0_0x127_0}, to_apply=%region_0.1 | reduce-window | flops 2080768 | bytes 131076 | tf_op jit(solution)/shard_map/reduce-window
  11.6 8.1 %scatter_custom_fusion.1 = s32[4096]{0:T(1024)S(1)} fusion(s32[2048]{0:T(1024)S(1)} %compare_select_fusion.1, s32[2048]{0:T(1024)S(1)} %iota.19, s32[]{:T(128)} %constant.38.clone.1), kind=kCustom, calls=%fused_computation.60 | custom fusion | bytes 16388 | tf_op jit(solution)/shard_map/scatter | solution.py:53
  19.7 23.0 %gather_fusion.1 = s32[4096]{0:T(1024)S(1)} fusion(s32[2048]{0:T(1024)S(1)} %copy-done.1, s32[4096]{0:T(1024)S(1)} %fusion.23), kind=kCustom, calls=%fused_computation.1 | custom fusion | bytes 49152 | tf_op jit(solution)/shard_map/gather | solution.py:56
  42.8 9.1 %scatter_custom_fusion = pred[4096]{0:T(1024)(128)(4,1)S(1)} fusion(s32[2048]{0:T(1024)S(1)} %compare_select_fusion.1, pred[2048]{0:T(1024)(128)(4,1)S(1)} %broadcast.124, pred[]{:T(512)} %constant.30.clone.1), kind=kCustom, calls=%fused_computation.64 | custom fusion | bytes 4097 | tf_op jit(solution)/shard_map/scatter | solution.py:55
  52.5 7.3 %all-to-all-start.1 = ((s32[1,8,512]{2,0,1:T(1,128)}), s32[1,8,512]{2,0,1:T(1,128)S(1)}, u32[]{:S(2)}, u32[]{:S(2)}) async-start(s32[1,8,512]{2,0,1:T(1,128)} %bitcast.8), calls=%async_computation.1 | async-start | bytes 32768 | tf_op jit(solution)/shard_map/all_to_all | solution.py:65
  61.9 12.1 %gather_fusion = bf16[4096,67]{1,0:T(8,128)(2,1)S(1)} fusion(bf16[67,2048]{0,1:T(8,128)(2,1)S(1)} %pad_maximum_fusion, s32[4096]{0:T(1024)S(1)} %fusion.23), kind=kCustom, calls=%fused_computation | custom fusion | bytes 1114112 | tf_op jit(solution)/shard_map/jit(_take)/gather | solution.py:61
  74.7 0.9 select_select_fusion
  75.6 6.0 %all-to-all-start = ((bf16[67,8,512]{2,0,1:T(8,128)(2,1)}), bf16[67,8,512]{2,0,1:T(8,128)(2,1)S(1)}, u32[]{:S(2)}, u32[]{:S(2)}) async-start(bf16[67,8,512]{2,0,1:T(8,128)(2,1)} %select_select_fusion), calls=%async_computation | async-start | bytes 1179648 | tf_op jit(solution)/shard_map/all_to_all | solution.py:64
  81.6 0.9 iota_compare_fusion.7
  82.5 14.4 %all-to-all-done = bf16[67,8,512]{2,0,1:T(8,128)(2,1)S(1)} async-done(((bf16[67,8,512]{2,0,1:T(8,128)(2,1)}), bf16[67,8,512]{2,0,1:T(8,128)(2,1)S(1)}, u32[]{:S(2)}, u32[]{:S(2)}) %all-to-all-start) | async-done | bytes 548896 | tf_op jit(solution)/shard_map/all_to_all | solution.py:64
  97.1 13.2 %fusion.9 = bf16[1536,128]{1,0:T(8,128)(2,1)S(1)} fusion(bf16[64,4096]{1,0:T(8,128)(2,1)S(1)} %bitcast.118, bf16[64,1536]{1,0:T(8,128)(2,1)S(1)} %copy-done, f32[4096]{0:T(1024)S(1)} %bitcast.123, f32[4096]{0:T(1024)S(1)} %bitcast.124, f32[4096]{0:T(1024)S(1)} %bitcast.122, pred[4096,128]{1,0:T(32,128)(4,1)S(1)} %iota_compare_fusion.7), kind=kOutput, calls=%fused_computation.16 | convolution fusion | flops 2447769600 | bytes 1687552 | tf_op jit(solution)/shard_map/dot_general | solution.py:73
  110.3 1.5 collective-permute-start
  111.8 10.3 %collective-permute-done = bf16[1536,128]{1,0:T(8,128)(2,1)S(1)} collective-permute-done((bf16[1536,128]{1,0:T(8,128)(2,1)S(1)}, bf16[1536,128]{1,0:T(8,128)(2,1)S(1)}, u32[]{:S(2)}, u32[]{:S(2)}) %collective-permute-start) | collective-permute-done | bytes 393248 | tf_op jit(solution)/shard_map/ppermute | solution.py:23
  122.1 4.7 %collective-permute-start.4 = (bf16[1536,128]{1,0:T(8,128)(2,1)S(1)}, bf16[1536,128]{1,0:T(8,128)(2,1)S(1)}, u32[]{:S(2)}, u32[]{:S(2)}) collective-permute-start(bf16[1536,128]{1,0:T(8,128)(2,1)S(1)} %fusion.9), channel_id=1, source_target_pairs={{0,7},{1,0},{2,1},{3,2},{4,3},{5,4},{6,5},{7,6},{8,15},{9,8},{10,9... | collective-permute-start | bytes 1179656 | tf_op jit(solution)/shard_map/ppermute | solution.py:24
  126.9 9.9 %collective-permute-done.1 = bf16[1536,128]{1,0:T(8,128)(2,1)S(1)} collective-permute-done((bf16[1536,128]{1,0:T(8,128)(2,1)S(1)}, bf16[1536,128]{1,0:T(8,128)(2,1)S(1)}, u32[]{:S(2)}, u32[]{:S(2)}) %collective-permute-start.1) | collective-permute-done | bytes 393248 | tf_op jit(solution)/shard_map/ppermute | solution.py:23
  136.8 2.5 %collective-permute-start.2 = (bf16[1536,128]{1,0:T(8,128)(2,1)S(1)}, bf16[1536,128]{1,0:T(8,128)(2,1)S(1)}, u32[]{:S(2)}, u32[]{:S(2)}) collective-permute-start(bf16[1536,128]{1,0:T(8,128)(2,1)S(1)} %collective-permute-done.1), channel_id=1, source_target_pairs={{0,1},{1,2},{2,3},{3,4},{4,5},{5,6},{6,7},{7,0},{8,9},{9,10},{10,1... | collective-permute-start | bytes 1179656 | tf_op jit(solution)/shard_map/ppermute | solution.py:23
  139.3 2.6 %collective-permute-start.5 = (bf16[1536,128]{1,0:T(8,128)(2,1)S(1)}, bf16[1536,128]{1,0:T(8,128)(2,1)S(1)}, u32[]{:S(2)}, u32[]{:S(2)}) collective-permute-start(bf16[1536,128]{1,0:T(8,128)(2,1)S(1)} %collective-permute-done.4), channel_id=1, source_target_pairs={{0,7},{1,0},{2,1},{3,2},{4,3},{5,4},{6,5},{7,6},{8,15},{9,8},{10,9... | collective-permute-start | bytes 1179656 | tf_op jit(solution)/shard_map/ppermute | solution.py:24
  141.9 12.9 %collective-permute-done.2 = bf16[1536,128]{1,0:T(8,128)(2,1)S(1)} collective-permute-done((bf16[1536,128]{1,0:T(8,128)(2,1)S(1)}, bf16[1536,128]{1,0:T(8,128)(2,1)S(1)}, u32[]{:S(2)}, u32[]{:S(2)}) %collective-permute-start.2) | collective-permute-done | bytes 393248 | tf_op jit(solution)/shard_map/ppermute | solution.py:23
  154.9 2.5 %collective-permute-start.3 = (bf16[1536,128]{1,0:T(8,128)(2,1)S(1)}, bf16[1536,128]{1,0:T(8,128)(2,1)S(1)}, u32[]{:S(2)}, u32[]{:S(2)}) collective-permute-start(bf16[1536,128]{1,0:T(8,128)(2,1)S(1)} %collective-permute-done.2), channel_id=1, source_target_pairs={{0,1},{1,2},{2,3},{3,4},{4,5},{5,6},{6,7},{7,0},{8,9},{9,10},{10,1... | collective-permute-start | bytes 1179656 | tf_op jit(solution)/shard_map/ppermute | solution.py:23
  157.4 2.3 %collective-permute-start.6 = (bf16[1536,128]{1,0:T(8,128)(2,1)S(1)}, bf16[1536,128]{1,0:T(8,128)(2,1)S(1)}, u32[]{:S(2)}, u32[]{:S(2)}) collective-permute-start(bf16[1536,128]{1,0:T(8,128)(2,1)S(1)} %collective-permute-done.5), channel_id=1, source_target_pairs={{0,7},{1,0},{2,1},{3,2},{4,3},{5,4},{6,5},{7,6},{8,15},{9,8},{10,9... | collective-permute-start | bytes 1179656 | tf_op jit(solution)/shard_map/ppermute | solution.py:24
  159.7 13.3 %collective-permute-done.3 = bf16[1536,128]{1,0:T(8,128)(2,1)S(1)} collective-permute-done((bf16[1536,128]{1,0:T(8,128)(2,1)S(1)}, bf16[1536,128]{1,0:T(8,128)(2,1)S(1)}, u32[]{:S(2)}, u32[]{:S(2)}) %collective-permute-start.3) | collective-permute-done | bytes 393248 | tf_op jit(solution)/shard_map/ppermute | solution.py:23
  176.0 1.4 gather_fusion.2
  177.4 21.3 %reduce-scatter.2.cloned.1.call-done = f32[256,128]{1,0:T(8,128)} async-done(((f32[1024,128]{1,0:T(8,128)}), f32[256,128]{1,0:T(8,128)}) %reduce-scatter.2.cloned.1.call-update) | async-done | bytes 131088 | tf_op jit(solution)/shard_map/reduce_scatter | solution.py:77
  198.6 1.6 broadcast_multiply_fusion
  (56 shorter events, 8.5 us)
Async XLA Ops:
  7.2 89.9 %copy-start = (bf16[64,1536]{1,0:T(8,128)(2,1)S(1)}, bf16[64,1536]{1,0:T(8,128)(2,1)}, u32[]{:S(2)}) copy-start(bf16[64,1536]{1,0:T(8,128)(2,1)} %param.6) | copy-start | bytes 589828
  7.2 12.5 %copy-start.1 = (s32[2048]{0:T(1024)S(1)}, s32[2048]{0:T(1024)}, u32[]{:S(2)}) copy-start(s32[2048]{0:T(1024)} %param.11) | copy-start | bytes 24580
  19.7 40.2 %copy-start.4 = (bf16[2048]{0:T(1024)(128)(2,1)S(1)}, bf16[2048]{0:T(1024)(128)(2,1)}, u32[]{:S(2)}) copy-start(bf16[2048]{0:T(1024)(128)(2,1)} %param.10) | copy-start | bytes 12292
  19.7 40.5 %copy-start.5 = (bf16[2048]{0:T(1024)(128)(2,1)S(1)}, bf16[2048]{0:T(1024)(128)(2,1)}, u32[]{:S(2)}) copy-start(bf16[2048]{0:T(1024)(128)(2,1)} %param.9) | copy-start | bytes 12292
  42.7 17.8 %copy-start.6 = (bf16[2048]{0:T(1024)(128)(2,1)S(1)}, bf16[2048]{0:T(1024)(128)(2,1)}, u32[]{:S(2)}) copy-start(bf16[2048]{0:T(1024)(128)(2,1)} %param.8) | copy-start | bytes 12292
  42.7 18.2 %copy-start.3 = (bf16[64,2048]{1,0:T(8,128)(2,1)S(1)}, bf16[64,2048]{1,0:T(8,128)(2,1)}, u32[]{:S(2)}) copy-start(bf16[64,2048]{1,0:T(8,128)(2,1)} %param.7) | copy-start | bytes 786436
  52.5 23.1 %all-to-all-start.1 = ((s32[1,8,512]{2,0,1:T(1,128)}), s32[1,8,512]{2,0,1:T(1,128)S(1)}, u32[]{:S(2)}, u32[]{:S(2)}) async-start(s32[1,8,512]{2,0,1:T(1,128)} %bitcast.8), calls=%async_computation.1 | async-start | bytes 32768 | tf_op jit(solution)/shard_map/all_to_all | solution.py:65
  75.6 21.4 %all-to-all-start = ((bf16[67,8,512]{2,0,1:T(8,128)(2,1)}), bf16[67,8,512]{2,0,1:T(8,128)(2,1)S(1)}, u32[]{:S(2)}, u32[]{:S(2)}) async-start(bf16[67,8,512]{2,0,1:T(8,128)(2,1)} %select_select_fusion), calls=%async_computation | async-start | bytes 1179648 | tf_op jit(solution)/shard_map/all_to_all | solution.py:64
  81.6 117.1 %reduce-scatter.2.cloned.1.call-start = ((), (), s32[]{:S(2)}) async-start(), calls=%async_computation.3 | async-start | bytes 655360 | tf_op jit(solution)/shard_map/reduce_scatter | solution.py:77
  110.3 65.3 %copy-start.2 = (bf16[1536,128]{1,0:T(8,128)(2,1)}, bf16[1536,128]{1,0:T(8,128)(2,1)S(1)}, u32[]{:S(2)}) copy-start(bf16[1536,128]{1,0:T(8,128)(2,1)S(1)} %fusion.9) | copy-start | bytes 1179652
  110.3 11.8 %collective-permute-start = (bf16[1536,128]{1,0:T(8,128)(2,1)S(1)}, bf16[1536,128]{1,0:T(8,128)(2,1)S(1)}, u32[]{:S(2)}, u32[]{:S(2)}) collective-permute-start(bf16[1536,128]{1,0:T(8,128)(2,1)S(1)} %fusion.9), channel_id=1, source_target_pairs={{0,1},{1,2},{2,3},{3,4},{4,5},{5,6},{6,7},{7,0},{8,9},{9,10},{10,1... | collective-permute-start | bytes 1179656 | tf_op jit(solution)/shard_map/ppermute | solution.py:23
  122.1 14.7 %collective-permute-start.1 = (bf16[1536,128]{1,0:T(8,128)(2,1)S(1)}, bf16[1536,128]{1,0:T(8,128)(2,1)S(1)}, u32[]{:S(2)}, u32[]{:S(2)}) collective-permute-start(bf16[1536,128]{1,0:T(8,128)(2,1)S(1)} %collective-permute-done), channel_id=1, source_target_pairs={{0,1},{1,2},{2,3},{3,4},{4,5},{5,6},{6,7},{7,0},{8,9},{9,10},{10,1... | collective-permute-start | bytes 1179656 | tf_op jit(solution)/shard_map/ppermute | solution.py:23
  122.1 17.1 %collective-permute-start.4 = (bf16[1536,128]{1,0:T(8,128)(2,1)S(1)}, bf16[1536,128]{1,0:T(8,128)(2,1)S(1)}, u32[]{:S(2)}, u32[]{:S(2)}) collective-permute-start(bf16[1536,128]{1,0:T(8,128)(2,1)S(1)} %fusion.9), channel_id=1, source_target_pairs={{0,7},{1,0},{2,1},{3,2},{4,3},{5,4},{6,5},{7,6},{8,15},{9,8},{10,9... | collective-permute-start | bytes 1179656 | tf_op jit(solution)/shard_map/ppermute | solution.py:24
  136.8 18.0 %collective-permute-start.2 = (bf16[1536,128]{1,0:T(8,128)(2,1)S(1)}, bf16[1536,128]{1,0:T(8,128)(2,1)S(1)}, u32[]{:S(2)}, u32[]{:S(2)}) collective-permute-start(bf16[1536,128]{1,0:T(8,128)(2,1)S(1)} %collective-permute-done.1), channel_id=1, source_target_pairs={{0,1},{1,2},{2,3},{3,4},{4,5},{5,6},{6,7},{7,0},{8,9},{9,10},{10,1... | collective-permute-start | bytes 1179656 | tf_op jit(solution)/shard_map/ppermute | solution.py:23
  139.3 18.1 %collective-permute-start.5 = (bf16[1536,128]{1,0:T(8,128)(2,1)S(1)}, bf16[1536,128]{1,0:T(8,128)(2,1)S(1)}, u32[]{:S(2)}, u32[]{:S(2)}) collective-permute-start(bf16[1536,128]{1,0:T(8,128)(2,1)S(1)} %collective-permute-done.4), channel_id=1, source_target_pairs={{0,7},{1,0},{2,1},{3,2},{4,3},{5,4},{6,5},{7,6},{8,15},{9,8},{10,9... | collective-permute-start | bytes 1179656 | tf_op jit(solution)/shard_map/ppermute | solution.py:24
  154.9 18.1 %collective-permute-start.3 = (bf16[1536,128]{1,0:T(8,128)(2,1)S(1)}, bf16[1536,128]{1,0:T(8,128)(2,1)S(1)}, u32[]{:S(2)}, u32[]{:S(2)}) collective-permute-start(bf16[1536,128]{1,0:T(8,128)(2,1)S(1)} %collective-permute-done.2), channel_id=1, source_target_pairs={{0,1},{1,2},{2,3},{3,4},{4,5},{5,6},{6,7},{7,0},{8,9},{9,10},{10,1... | collective-permute-start | bytes 1179656 | tf_op jit(solution)/shard_map/ppermute | solution.py:23
  157.4 18.3 %collective-permute-start.6 = (bf16[1536,128]{1,0:T(8,128)(2,1)S(1)}, bf16[1536,128]{1,0:T(8,128)(2,1)S(1)}, u32[]{:S(2)}, u32[]{:S(2)}) collective-permute-start(bf16[1536,128]{1,0:T(8,128)(2,1)S(1)} %collective-permute-done.5), channel_id=1, source_target_pairs={{0,7},{1,0},{2,1},{3,2},{4,3},{5,4},{6,5},{7,6},{8,15},{9,8},{10,9... | collective-permute-start | bytes 1179656 | tf_op jit(solution)/shard_map/ppermute | solution.py:24
Sparse Core Ops, SparseCore 0:
  177.5 21.1 reduce-scatter.1
